TPU v7x, 32 devices: a whole 2x2x4 slice. The times are simulated.
32 devices in a mesh: slab: 4 (over y, x), space: 8 (over z, core).
Axes of the slice: x: 2, y: 2, z: 4, core: 2. Of those that a mesh axis runs over, the one named last changes fastest.
Arguments:
- dipoles: float32 [3, 16384], P(None, ('slab', 'space')), may hold values from -3 to 3
- residual: float32 [3, 16384], P(None, ('slab', 'space')), may hold values from -12 to 12, as said below
- cells: int32 [3, 16384], P(None, ('slab', 'space')), may hold values from 0 to 255, as said below
- fraction: float32 [3, 16384], P(None, ('slab', 'space')), may hold values from 0.25 to 0.75
- polarizability: float32 [16384], P(('slab', 'space')), may hold values from 0.3 to 2.5
- tile_order: int32 [32, 512], P(('slab', 'space')), may hold values from 0 to 511, as said below
- send_tiles: int32 [32, 2], P(('slab', 'space')), may hold values from 0 to 3, as said below
- tile_lists: int32 [32, 4, 8], P(('slab', 'space')), may hold values from 0 to 19, as said below
- tile_counts: int32 [32, 4], P(('slab', 'space')), may hold values from 1 to 8, as said below
Outputs:
- dipoles_next: float32 [3, 16384], P(None, ('slab', 'space'))
- residual_next: float32 [3, 16384], P(None, ('slab', 'space'))
- direction: float32 [3, 16384], P(None, ('slab', 'space'))
Inputs may be any that keep to these rules, and one draw needn't show every extreme that they name: The residual's entries stay within the stated range. `cells`: the first component is below 64 and the second below 32; no two atoms of one device share a cell. `tile_order`: each device's row holds every number of 0 to 511 once. `send_tiles`: the 2 tile numbers of each device are distinct. `tile_lists`: entry 0 of the list of tile t is t itself; the 8 entries of one list are distinct. `tile_counts`: on some devices every tile has 8 live entries.
All inputs are finite; a program needn't handle non-finite values.
Results may differ from a plain program's by a relative error of at most 0.0003.
Values sent between devices are 32-bit elements; how exact they have to be, the bound alone decides.
A program may use at most 128 MiB of HBM per device.

v0:
```python
import math

import jax
import jax.numpy as jnp
from jax import lax
from jax.sharding import PartitionSpec as P

G = 256


EWALD_BETA = 0.4
THOLE_SCALE = 0.39
SELF_FIELD = 4.0 * EWALD_BETA**3 / (3.0 * math.sqrt(math.pi))
HIGHEST = lax.Precision.HIGHEST


def with_halo(array, sides, width):
    for axis, dim in sides:
        devices, length = (lax.axis_size(axis), array.shape[dim])
        up = [(i, (i + 1) % devices) for i in range(devices)]
        down = [(j, i) for i, j in up]
        last = lax.slice_in_dim(array, length - width, length, axis=dim)
        initial = lax.slice_in_dim(array, 0, width, axis=dim)
        before = lax.ppermute(last, axis, up)
        after = lax.ppermute(initial, axis, down)
        array = jnp.concatenate([before, array, after], axis=dim)
    return array


def spline(fraction):
    centre_arg = fraction - 0.5
    lower_one = fraction + 0.5
    upper_one = 1.5 - fraction
    lower_two = fraction + 1.5
    upper_two = 2.5 - fraction

    def middle(amount):
        return (
            55.0 + 20.0 * amount - 120.0 * amount**2 + 80.0 * amount**3 - 16.0 * amount**4
        ) / 96.0

    def middle_slope(amount):
        return (20.0 - 240.0 * amount + 240.0 * amount**2 - 64.0 * amount**3) / 96.0

    def outer_piece(amount):
        return (5.0 - 2.0 * amount) ** 4 / 384.0

    def outer_slope(amount):
        return -((5.0 - 2.0 * amount) ** 3) / 48.0

    centre = 115.0 / 192.0 - 0.625 * centre_arg**2 + 0.25 * centre_arg**4
    centre_slope = -1.25 * centre_arg + centre_arg**3
    weights = jnp.stack(
        [
            outer_piece(lower_two),
            middle(lower_one),
            centre,
            middle(upper_one),
            outer_piece(upper_two),
        ]
    )
    slopes = jnp.stack(
        [
            outer_slope(lower_two),
            middle_slope(lower_one),
            centre_slope,
            -middle_slope(upper_one),
            -outer_slope(upper_two),
        ]
    )
    return (weights, slopes)


def wave_factors(freq_ids):
    wrapped = jnp.where(freq_ids > G // 2, freq_ids - G, freq_ids).astype(jnp.float32) / G
    angles = 2.0 * math.pi / G * freq_ids.astype(jnp.float32)
    modulus = 115.0 / 192.0 + 19.0 / 48.0 * jnp.cos(angles) + 1.0 / 192.0 * jnp.cos(2.0 * angles)
    return (
        wrapped * wrapped,
        jnp.exp(-((math.pi / EWALD_BETA) ** 2) * wrapped * wrapped) / (modulus * modulus),
    )


def multiplier(freq_x, freq_y, freq_z):
    square_x, factor_x = wave_factors(freq_x)
    square_y, factor_y = wave_factors(freq_y)
    square_z, factor_z = wave_factors(freq_z)
    square_sum = square_x + square_y + square_z
    anchor = ((freq_x == 0) & (freq_y == 0) & (freq_z == 0)).astype(jnp.float32)
    return (
        (1.0 - anchor)
        * factor_x
        * factor_y
        * factor_z
        / (math.pi * float(G) ** 3 * (square_sum + anchor))
    )


def separation(own_tile, geometry):
    displacement = geometry[:, :3, None, :] - own_tile[None, :3, :, None]
    half_box = 0.5 * G
    depth_z = displacement[:, 2]
    depth_z = jnp.where(
        depth_z > half_box, depth_z - G, jnp.where(depth_z < -half_box, depth_z + G, depth_z)
    )
    return jnp.stack([displacement[:, 0], displacement[:, 1], depth_z], 1)


def grouped(values, group_count):
    return values.reshape((group_count, -1) + values.shape[1:])


def pair_coefficients(own_geometry, pool_geometry, neighbour_ids, neighbour_counts):
    count_tiles = own_geometry.shape[0]
    tile_width = own_geometry.shape[2]
    slots = neighbour_ids.shape[1]
    group_count = count_tiles // math.gcd(count_tiles, 4)
    tile_ids = jnp.arange(count_tiles, dtype=jnp.int32)
    diagonal = (jnp.arange(tile_width)[:, None] == jnp.arange(tile_width)[None, :]).astype(
        jnp.float32
    )
    slot_ids = jnp.arange(slots, dtype=jnp.int32)

    def pair_per_tile(tile_id, own_tile, picked, live_count):
        geometry = pool_geometry[picked]
        displacement = separation(own_tile, geometry)
        itself = (picked == tile_id).astype(jnp.float32)[:, None, None] * diagonal[None]
        square = jnp.sum(displacement * displacement, 1) + itself
        distance = jnp.sqrt(square)
        inverse = 1.0 / distance
        inverse_sq = inverse * inverse
        gauss = jnp.exp(-(EWALD_BETA**2) * square)
        bare_zero = lax.erfc(EWALD_BETA * distance) * inverse
        bare_one = (bare_zero + 2.0 * EWALD_BETA / math.sqrt(math.pi) * gauss) * inverse_sq
        bare_two = (3.0 * bare_one + 4.0 * EWALD_BETA**3 / math.sqrt(math.pi) * gauss) * inverse_sq
        damping = (
            THOLE_SCALE
            * square
            * distance
            * lax.rsqrt(own_tile[3][None, :, None] * geometry[:, 3][:, None, :])
        )
        decay = jnp.exp(-damping)
        rank_three = bare_one - decay * inverse * inverse_sq
        rank_five = bare_two - 3.0 * (1.0 + damping) * decay * inverse * inverse_sq * inverse_sq
        weight_pair = (slot_ids < live_count).astype(jnp.float32)[:, None, None] * (1.0 - itself)
        return (weight_pair * rank_five, weight_pair * rank_three)

    def pair_per_group(inputs):
        return jax.vmap(pair_per_tile)(*inputs)

    fives, threes = lax.map(
        pair_per_group,
        (
            grouped(tile_ids, group_count),
            grouped(own_geometry, group_count),
            grouped(neighbour_ids, group_count),
            grouped(neighbour_counts, group_count),
        ),
    )
    return (
        fives.reshape((count_tiles,) + fives.shape[2:]),
        threes.reshape((count_tiles,) + threes.shape[2:]),
    )


def short_field(own_geometry, pool_geometry, pool_dipoles, neighbour_ids, coefficients):
    count_tiles = own_geometry.shape[0]
    group_count = count_tiles // math.gcd(count_tiles, 4)
    fives, threes = coefficients

    def short_per_tile(own_tile, picked, rank_five, rank_three):
        geometry = pool_geometry[picked]
        dipole = pool_dipoles[picked]
        displacement = separation(own_tile, geometry)
        projection = jnp.sum(displacement * dipole[:, :, None, :], 1)
        terms = (
            rank_five[:, None] * displacement * projection[:, None]
            - rank_three[:, None] * dipole[:, :, None, :]
        )
        return jnp.sum(terms, (0, 3))

    def short_per_group(inputs):
        return jax.vmap(short_per_tile)(*inputs)

    fields = lax.map(
        short_per_group,
        (
            grouped(own_geometry, group_count),
            grouped(neighbour_ids, group_count),
            grouped(fives, group_count),
            grouped(threes, group_count),
        ),
    )
    return fields.reshape((count_tiles,) + fields.shape[2:])


def fold_rims(padded, axis_id, length):
    core = lax.slice_in_dim(padded, 4, length + 4, axis=axis_id)
    lower_rim = lax.slice_in_dim(padded, 0, 2, axis=axis_id)
    upper_rim = lax.slice_in_dim(padded, length + 6, length + 8, axis=axis_id)
    lower_pad = [(0, 0)] * padded.ndim
    lower_pad[axis_id] = (0, length - 2)
    upper_pad = [(0, 0)] * padded.ndim
    upper_pad[axis_id] = (length - 2, 0)
    return core + jnp.pad(lower_rim, lower_pad) + jnp.pad(upper_rim, upper_pad)


def to_tiles(values, count_tiles):
    return values.reshape(values.shape[0], count_tiles, -1).transpose(1, 0, 2)


def from_tiles(tile_values):
    return tile_values.transpose(1, 0, 2).reshape(tile_values.shape[1], -1)


def tile_rims(payload):
    return with_halo(payload, (("slab", 0), ("space", 1)), 1)


def grid_rims(values):
    return with_halo(values, (("slab", 0), ("space", 1)), 2)


def pool_from(received):
    flattened = received.reshape((9,) + received.shape[2:])
    picked = flattened[jnp.array([0, 1, 2, 3, 5, 6, 7, 8], dtype=jnp.int32)]
    return picked.reshape((-1,) + received.shape[3:])


def point_tables(cell_row, frac_row, length, wrapped):
    weights, slopes = spline(frac_row)
    step_ids = jnp.arange(5, dtype=jnp.int32)[:, None]
    if wrapped:
        targets = (cell_row[None] + step_ids - 2 + length) % length
    else:
        targets = cell_row[None] + step_ids
    matches = (jnp.arange(length, dtype=jnp.int32)[:, None, None] == targets[None]).astype(
        jnp.float32
    )
    return (jnp.sum(matches * weights[None], 1), jnp.sum(matches * slopes[None], 1))


def local(
    dipoles,
    residual,
    cells,
    fraction,
    polarizability,
    tile_order,
    send_tiles,
    tile_lists,
    tile_counts,
):
    atom_order = tile_order[0]
    sending = send_tiles[0]
    neighbour_ids = tile_lists[0]
    counts = tile_counts[0]
    count_tiles = neighbour_ids.shape[0]
    atom_count = atom_order.shape[0]
    send_count = sending.shape[0]
    n_slab = lax.axis_size("slab")
    n_space = lax.axis_size("space")
    extent_x = G // n_slab
    extent_y = G // n_space
    extent_k = G // n_space
    extent_w = G // n_slab
    slab_index = lax.axis_index("slab")
    space_index = lax.axis_index("space")
    cell_rows = cells[:, atom_order]
    frac_rows = fraction[:, atom_order]
    alphas = polarizability[atom_order][None]
    target = residual[:, atom_order]
    moments = dipoles[:, atom_order]
    positions = cell_rows.astype(jnp.float32) + frac_rows
    geometry = to_tiles(jnp.concatenate([positions, alphas], 0), count_tiles)
    shift_rows = []
    for step_a in range(3):
        for step_b in range(3):
            if step_a != 1 or step_b != 1:
                shift_rows.append(
                    [float((step_a - 1) * extent_x), float((step_b - 1) * extent_y), 0.0, 0.0]
                )
    shifts = jnp.repeat(jnp.array(shift_rows, jnp.float32), send_count, 0)[:, :, None]
    search = alphas * target
    search_tiles = to_tiles(search, count_tiles)
    first_pool = pool_from(
        tile_rims(jnp.concatenate([geometry, search_tiles], 1)[sending][None, None])
    )
    pool_geometry = jnp.concatenate([geometry, first_pool[:, :4] + shifts], 0)
    coefficients = pair_coefficients(geometry, pool_geometry, neighbour_ids, counts)

    def short_from(values_tiles, received_dipoles):
        pool_dipoles = jnp.concatenate([values_tiles, received_dipoles], 0)
        return from_tiles(
            short_field(geometry, pool_geometry, pool_dipoles, neighbour_ids, coefficients)
        )

    def short_apply(values):
        values_tiles = to_tiles(values, count_tiles)
        return short_from(values_tiles, pool_from(tile_rims(values_tiles[sending][None, None])))

    search = alphas * (target + short_from(search_tiles, first_pool[:, 4:]))
    for sweep_id in range(2):
        search = alphas * (target + short_apply(search))
    search_dot = jnp.sum(target * search)
    search_total = lax.psum(search_dot, ("slab", "space"))
    weight_x, slope_x = point_tables(cell_rows[0], frac_rows[0], extent_x + 4, False)
    weight_y, slope_y = point_tables(cell_rows[1], frac_rows[1], extent_y + 4, False)
    weight_z, slope_z = point_tables(cell_rows[2], frac_rows[2], G, True)
    plane_xs = (slope_x[:, None] * weight_y[None]).reshape(-1, atom_count)
    plane_ys = (weight_x[:, None] * slope_y[None]).reshape(-1, atom_count)
    plane_ww = (weight_x[:, None] * weight_y[None]).reshape(-1, atom_count)
    left_side = jnp.concatenate(
        [search[0][None] * plane_xs + search[1][None] * plane_ys, plane_ww], 1
    )
    right_side = jnp.concatenate([weight_z.T, (search[2][None] * slope_z).T], 0)
    spread = jnp.dot(left_side, right_side, precision=HIGHEST).reshape(
        extent_x + 4, extent_y + 4, G
    )
    planes = fold_rims(fold_rims(grid_rims(spread), 0, extent_x), 1, extent_y)
    grid_ids = jnp.arange(G, dtype=jnp.int32)
    angles = 2.0 * math.pi / G * (grid_ids[:, None] * grid_ids[None, :] % G).astype(jnp.float32)
    cas_table = jnp.cos(angles) + jnp.sin(angles)
    freq_z = space_index * extent_k + jnp.arange(extent_k, dtype=jnp.int32)
    along_z = jnp.einsum(
        "xvz,zsk->sxvk", planes, cas_table.reshape(G, n_space, extent_k), precision=HIGHEST
    )
    columns = lax.all_to_all(
        along_z.reshape(n_space, -1), "space", split_axis=0, concat_axis=0, tiled=True
    )
    columns = columns.reshape(n_space, extent_x, extent_y, extent_k)
    along_y = jnp.einsum(
        "sxvk,svtw->txkw",
        columns,
        cas_table.reshape(n_space, extent_y, n_slab, extent_w),
        precision=HIGHEST,
    )
    gathered_x = lax.all_to_all(
        along_y.reshape(n_slab, -1), "slab", split_axis=0, concat_axis=0, tiled=True
    )
    gathered_x = gathered_x.reshape(n_slab, extent_x, extent_k, extent_w)
    spectrum = jnp.einsum(
        "txkw,txm->kwm", gathered_x, cas_table.reshape(n_slab, extent_x, G), precision=HIGHEST
    )
    freq_y = slab_index * extent_w + jnp.arange(extent_w, dtype=jnp.int32)
    scaled = spectrum * multiplier(
        grid_ids[None, None, :], freq_y[None, :, None], freq_z[:, None, None]
    )
    back_x = jnp.einsum(
        "kwm,txm->txkw", scaled, cas_table.reshape(n_slab, extent_x, G), precision=HIGHEST
    )
    returned = lax.all_to_all(
        back_x.reshape(n_slab, -1), "slab", split_axis=0, concat_axis=0, tiled=True
    )
    returned = returned.reshape(n_slab, extent_x, extent_k, extent_w)
    planes_send = jnp.einsum(
        "txkw,twsv->sxvk",
        returned,
        cas_table.reshape(n_slab, extent_w, n_space, extent_y),
        precision=HIGHEST,
    )
    planes_back = lax.all_to_all(
        planes_send.reshape(n_space, -1), "space", split_axis=0, concat_axis=0, tiled=True
    )
    planes_back = planes_back.reshape(n_space, extent_x, extent_y, extent_k)
    potential = jnp.einsum(
        "sxvk,skz->xvz", planes_back, cas_table.reshape(n_space, extent_k, G), precision=HIGHEST
    )
    beside_all = grid_rims(potential)
    probed = jnp.dot(
        beside_all.reshape(-1, G), jnp.concatenate([weight_z, slope_z], 1), precision=HIGHEST
    )
    probed_w = probed[:, :atom_count]
    probed_s = probed[:, atom_count:]
    recip_field = -jnp.stack(
        [
            jnp.sum(plane_xs * probed_w, 0),
            jnp.sum(plane_ys * probed_w, 0),
            jnp.sum(plane_ww * probed_s, 0),
        ]
    )
    applied = search / alphas - short_apply(search) - SELF_FIELD * search - recip_field
    curve_local = jnp.sum(search * applied)
    curve_total = lax.psum(curve_local, ("slab", "space"))
    step_size = search_total / curve_total

    def restore(values):
        return jnp.zeros_like(values).at[:, atom_order].set(values)

    return (
        restore(moments + step_size * search),
        restore(target - step_size * applied),
        restore(search),
    )


def solution(mesh):
    return jax.shard_map(
        local,
        mesh=mesh,
        in_specs=(
            P(None, ("slab", "space")),
            P(None, ("slab", "space")),
            P(None, ("slab", "space")),
            P(None, ("slab", "space")),
            P(("slab", "space")),
            P(("slab", "space"), None),
            P(("slab", "space"), None),
            P(("slab", "space"), None, None),
            P(("slab", "space"), None),
        ),
        out_specs=(
            P(None, ("slab", "space")),
            P(None, ("slab", "space")),
            P(None, ("slab", "space")),
        ),
        check_vma=False,
    )
```

profile of v0, /device:TPU:12, one launch (start us, length us, event | category | flops | bytes accessed | tf_op | source)
XLA Modules:
  0.0 580.0 jit_solution(2260438709515996948)
XLA Ops:
  29.3 7.3 %fusion.32 = (f32[4,8,128,128]{3,2,1,0:T(8,128)S(1)}, f32[4,8,128,128]{3,2,1,0:T(8,128)S(1)}) fusion(f32[4,8,128,128]{3,2,1,0:T(8,128)S(1)} %get-tuple-element.138, f32[4,8,128]{2,1,0:T(8,128)S(1)} %bitcast.243, f32[4,128]{1,0:T(4,128)S(1)} %bitcast.273, f32[128,128]{1,0:T(8,128)S(1)} %fusion.188, f32[4,8]{1,0:T(4,128)S(1)} %get-tuple-element.219, ...), kind=kLoop, calls=%fused_computation.82 | loop fusion | flops 46661632 | bytes 6375680 | tf_op jit(solution)/shard_map/while/body/eval_jaxpr/vmap()/mul | solution.py:146
  48.1 6.5 %broadcast_multiply_fusion = (f32[68,36,512]{2,1,0:T(8,128)}, f32[68,36,512]{2,1,0:T(8,128)}, f32[68,36,512]{2,1,0:T(8,128)}) fusion(f32[36,512]{1,0:T(8,128)S(1)} %get-tuple-element.156, f32[68,512]{1,0:T(8,128)S(1)} %get-tuple-element.155, f32[36,512]{1,0:T(8,128)S(1)} %get-tuple-element.157, f32[68,512]{1,0:T(8,128)S(1)} %get-tuple-element.154), kind=kLoop, calls=%fused_computation.57 | loop fusion | flops 3760128 | bytes 15466496 | tf_op jit(solution)/shard_map/mul | solution.py:311
  73.1 6.7 %mul.1445 = f32[2448,512]{1,0:T(8,128)} reshape(f32[68,36,512]{2,1,0:T(8,128)} %get-tuple-element.178) | data formatting | bytes 10027008 | tf_op jit(solution)/shard_map/mul | solution.py:311
  79.8 6.6 %mul.1448 = f32[2448,512]{1,0:T(8,128)} reshape(f32[68,36,512]{2,1,0:T(8,128)} %get-tuple-element.179) | data formatting | bytes 10027008 | tf_op jit(solution)/shard_map/mul | solution.py:312
  86.4 6.6 %mul.1382 = f32[2448,512]{1,0:T(8,128)} reshape(f32[68,36,512]{2,1,0:T(8,128)} %get-tuple-element.180) | data formatting | bytes 10027008 | tf_op jit(solution)/shard_map/mul | solution.py:310
  107.7 8.9 %fusion = f32[2448,256]{1,0:T(8,128)S(1)} fusion(f32[2448,512]{1,0:T(8,128)S(1)} %bitcast.220, f32[2448,512]{1,0:T(8,128)S(1)} %multiply_add_fusion, f32[512,256]{0,1:T(8,128)S(1)} %multiply_bitcast_fusion, f32[512,256]{0,1:T(8,128)S(1)} %bitcast.222), kind=kOutput, calls=%fused_computation.21 | convolution fusion | flops 7703511040 | bytes 13582336 | tf_op jit(solution)/shard_map/dot_general | solution.py:317
  134.4 8.1 %convolution_bitcast_fusion = f32[8,64,32,32]{1,3,2,0:T(8,128)} fusion(f32[64,32,256]{2,1,0:T(8,128)S(1)} %fusion.40, s32[8,32]{1,0:T(8,128)S(1)} %multiply_add_fusion.2), kind=kOutput, calls=%fused_computation.69 | convolution fusion | flops 1611595776 | bytes 4195328 | tf_op jit(solution)/shard_map/xvz,zsk->sxvk/dot_general | solution.py:325
  142.5 9.1 %copy.366 = f32[8,64,32,32]{3,2,1,0:T(8,128)} copy(f32[8,64,32,32]{1,3,2,0:T(8,128)} %convolution_bitcast_fusion) | data formatting | bytes 4194304 | tf_op jit(solution)/shard_map/xvz,zsk->sxvk/transpose | solution.py:325
  151.7 8.6 %all_to_all.32 = f32[8,1,65536]{2,1,0:T(1,128)} reshape(f32[8,64,32,32]{3,2,1,0:T(8,128)} %copy.366) | data formatting | bytes 4194304 | tf_op jit(solution)/shard_map/all_to_all | solution.py:328
  160.2 11.3 %all-to-all-start = ((f32[8,1,65536]{2,1,0:T(1,128)}), f32[8,1,65536]{2,1,0:T(1,128)}, u32[]{:S(2)}, u32[]{:S(2)}) async-start(f32[8,1,65536]{2,1,0:T(1,128)} %all_to_all.32), calls=%async_computation | async-start | bytes 4194304 | tf_op jit(solution)/shard_map/all_to_all | solution.py:328
  171.6 45.5 %all-to-all-done = f32[8,1,65536]{2,1,0:T(1,128)} async-done(((f32[8,1,65536]{2,1,0:T(1,128)}), f32[8,1,65536]{2,1,0:T(1,128)}, u32[]{:S(2)}, u32[]{:S(2)}) %all-to-all-start) | async-done | bytes 2097184 | tf_op jit(solution)/shard_map/all_to_all | solution.py:328
  217.1 7.9 %reduce.5 = f32[8,65536]{1,0:T(8,128)} reduce(f32[8,1,65536]{2,1,0:T(1,128)} %all-to-all-done, f32[]{:T(128)} %constant.439), dimensions={1}, to_apply=%all_to_all.25.reduce_sub_computation | reduce | bytes 4194308 | tf_op jit(solution)/shard_map/all_to_all | solution.py:328
  224.9 7.5 %reshape.754 = f32[8,64,32,32]{3,2,1,0:T(8,128)} reshape(f32[8,65536]{1,0:T(8,128)} %reduce.5) | data formatting | bytes 4194304 | tf_op jit(solution)/shard_map/reshape | solution.py:331
  232.5 8.9 %copy.368 = f32[8,64,32,32]{1,2,0,3:T(8,128)} copy(f32[8,64,32,32]{3,2,1,0:T(8,128)} %reshape.754) | data formatting | bytes 4194304 | tf_op jit(solution)/shard_map/reshape | solution.py:331
  241.4 10.1 %fusion.14 = f32[4,64,32,64]{1,3,2,0:T(8,128)} fusion(f32[8,64,32,32]{1,2,0,3:T(8,128)} %copy.368, s32[4,64]{1,0:T(4,128)S(1)} %multiply_add_fusion.5, s32[8,32]{1,0:T(8,128)S(1)} %multiply_add_fusion.2), kind=kOutput, calls=%fused_computation.70 | convolution fusion | flops 1611595776 | bytes 4196352 | tf_op jit(solution)/shard_map/sxvk,svtw->txkw/dot_general | solution.py:332
  269.1 24.1 %all-to-all-done.1 = f32[4,1,131072]{2,1,0:T(1,128)} async-done(((f32[4,1,131072]{2,1,0:T(1,128)}), f32[4,1,131072]{2,1,0:T(1,128)}, u32[]{:S(2)}, u32[]{:S(2)}) %all-to-all-start.1) | async-done | bytes 2097184 | tf_op jit(solution)/shard_map/all_to_all | solution.py:338
  293.2 8.4 %reduce.6 = f32[4,131072]{1,0:T(4,128)} reduce(f32[4,1,131072]{2,1,0:T(1,128)} %all-to-all-done.1, f32[]{:T(128)} %constant.439), dimensions={1}, to_apply=%all_to_all.27.reduce_sub_computation | reduce | bytes 4194308 | tf_op jit(solution)/shard_map/all_to_all | solution.py:338
  307.1 11.7 %fusion.10 = f32[32,64,256,1]{2,1,3,0:T(8,128)S(1)} fusion(f32[4,64,32,64]{3,2,1,0:T(8,128)} %reshape.755, s32[4,64]{1,0:T(4,128)S(1)} %multiply_add_fusion.5), kind=kOutput, calls=%fused_computation.46 | convolution fusion | flops 1611595776 | bytes 4195328 | tf_op jit(solution)/shard_map/txkw,txm->kwm/dot_general | solution.py:342
  334.1 30.0 %all_to_all.40 = f32[4,1,131072]{2,1,0:T(1,128)} all-to-all(f32[4,1,131072]{2,1,0:T(1,128)} %all_to_all.34), channel_id=1, replica_groups=mesh['slab'=4,'space'=8] {'slab'}, dimensions={0} | all-to-all | bytes 4194304 | tf_op jit(solution)/shard_map/all_to_all | solution.py:352
  364.1 8.4 %reduce.7 = f32[4,131072]{1,0:T(4,128)} reduce(f32[4,1,131072]{2,1,0:T(1,128)} %all_to_all.40, f32[]{:T(128)} %constant.439), dimensions={1}, to_apply=%all_to_all.29.reduce_sub_computation | reduce | bytes 4194308 | tf_op jit(solution)/shard_map/all_to_all | solution.py:352
  378.0 16.0 %fusion.17 = f32[8,64,32,32]{1,2,3,0:T(8,128)} fusion(f32[4,64,32,64]{3,2,1,0:T(8,128)} %reshape.756, s32[8,32]{1,0:T(8,128)S(1)} %multiply_add_fusion.2, s32[4,64]{1,0:T(4,128)S(1)} %multiply_add_fusion.5), kind=kOutput, calls=%fused_computation.71 | convolution fusion | flops 1611595776 | bytes 4196352 | tf_op jit(solution)/shard_map/txkw,twsv->sxvk/dot_general | solution.py:356
  394.0 9.2 %copy.375 = f32[8,64,32,32]{3,2,1,0:T(8,128)} copy(f32[8,64,32,32]{1,2,3,0:T(8,128)} %fusion.17) | data formatting | bytes 4194304 | tf_op jit(solution)/shard_map/txkw,twsv->sxvk/transpose | solution.py:356
  403.1 8.6 %all_to_all.35 = f32[8,1,65536]{2,1,0:T(1,128)} reshape(f32[8,64,32,32]{3,2,1,0:T(8,128)} %copy.375) | data formatting | bytes 4194304 | tf_op jit(solution)/shard_map/all_to_all | solution.py:362
  411.7 7.0 %all-to-all-start.3 = ((f32[8,1,65536]{2,1,0:T(1,128)}), f32[8,1,65536]{2,1,0:T(1,128)}, u32[]{:S(2)}, u32[]{:S(2)}) async-start(f32[8,1,65536]{2,1,0:T(1,128)} %all_to_all.35), calls=%async_computation.3 | async-start | bytes 4194304 | tf_op jit(solution)/shard_map/all_to_all | solution.py:362
  429.4 10.2 %collective-permute-done.15 = f32[3,1,2,3,128]{4,3,2,1,0:T(4,128)S(1)} collective-permute-done((f32[3,1,2,3,128]{4,3,2,1,0:T(4,128)S(1)}, f32[3,1,2,3,128]{4,3,2,1,0:T(4,128)S(1)}, u32[]{:S(2)}, u32[]{:S(2)}) %collective-permute-start.15) | collective-permute-done | bytes 9248 | tf_op jit(solution)/shard_map/ppermute | solution.py:25
  439.6 14.5 %collective-permute-done.14 = f32[3,1,2,3,128]{4,3,2,1,0:T(4,128)S(1)} collective-permute-done((f32[3,1,2,3,128]{4,3,2,1,0:T(4,128)S(1)}, f32[3,1,2,3,128]{4,3,2,1,0:T(4,128)S(1)}, u32[]{:S(2)}, u32[]{:S(2)}) %collective-permute-start.14) | collective-permute-done | bytes 9248 | tf_op jit(solution)/shard_map/ppermute | solution.py:24
  455.4 9.1 %all-to-all-done.3 = f32[8,1,65536]{2,1,0:T(1,128)} async-done(((f32[8,1,65536]{2,1,0:T(1,128)}), f32[8,1,65536]{2,1,0:T(1,128)}, u32[]{:S(2)}, u32[]{:S(2)}) %all-to-all-start.3) | async-done | bytes 2097184 | tf_op jit(solution)/shard_map/all_to_all | solution.py:362
  464.5 7.9 %reduce.8 = f32[8,65536]{1,0:T(8,128)} reduce(f32[8,1,65536]{2,1,0:T(1,128)} %all-to-all-done.3, f32[]{:T(128)} %constant.439), dimensions={1}, to_apply=%all_to_all.31.reduce_sub_computation | reduce | bytes 4194308 | tf_op jit(solution)/shard_map/all_to_all | solution.py:362
  472.4 7.5 %reshape.757 = f32[8,64,32,32]{3,2,1,0:T(8,128)} reshape(f32[8,65536]{1,0:T(8,128)} %reduce.8) | data formatting | bytes 4194304 | tf_op jit(solution)/shard_map/reshape | solution.py:365
  479.9 9.4 %convolution_bitcast_fusion.1 = f32[64,32,256]{2,1,0:T(8,128)S(1)} fusion(f32[8,64,32,32]{3,2,1,0:T(8,128)} %reshape.757, s32[8,32]{1,0:T(8,128)S(1)} %multiply_add_fusion.2), kind=kOutput, calls=%fused_computation.113 | convolution fusion | flops 1611595776 | bytes 4195328 | tf_op jit(solution)/shard_map/sxvk,skz->xvz/dot_general | solution.py:366
  507.3 10.9 %fusion.54 = f32[2448,1024]{1,0:T(8,128)S(1)} fusion(f32[2448,256]{1,0:T(8,128)} %reshape.758, f32[256,512]{1,0:T(8,128)S(1)} %copy-done.16, f32[256,512]{1,0:T(8,128)S(1)} %copy-done.21), kind=kOutput, calls=%fused_computation.117 | convolution fusion | flops 7701004288 | bytes 13582336 | tf_op jit(solution)/shard_map/dot_general | solution.py:370
  524.2 47.2 %all-reduce.2 = (f32[]{:T(128)}, f32[]{:T(128)}) all-reduce(f32[]{:T(128)} %get-tuple-element.143, f32[]{:T(128)} %get-tuple-element.142), channel_id=1, replica_groups=mesh['slab'=4,'space'=8] {'slab','space'}, use_global_device_ids=true, to_apply=%region_8.9 | all-reduce | flops 2 | bytes 16 | tf_op jit(solution)/shard_map/psum | solution.py:306
  (270 shorter events, 176.8 us)
Async XLA Ops:
  2.9 18.0 %copy-start.27 = (f32[8,4]{1,0:T(8,128)S(1)}, f32[8,4]{1,0:T(8,128)}, u32[]{:S(2)}) copy-start(f32[8,4]{1,0:T(8,128)} %constant.421.clone) | copy-start | bytes 388
  10.9 3.7 collective-permute-start.1
  12.4 4.5 collective-permute-start
  16.9 1.5 collective-permute-start.3
  16.9 3.3 collective-permute-start.2
  42.7 3.6 collective-permute-start.5
  42.9 4.5 collective-permute-start.4
  47.4 7.2 %collective-permute-start.7 = (f32[3,1,2,3,128]{4,3,2,1,0:T(4,128)S(1)}, f32[3,1,2,3,128]{4,3,2,1,0:T(4,128)S(1)}, u32[]{:S(2)}, u32[]{:S(2)}) collective-permute-start(f32[3,1,2,3,128]{4,3,2,1,0:T(4,128)S(1)} %pad_maximum_fusion.17), channel_id=1, source_target_pairs={{1,0},{2,1},{3,2},{4,3},{5,4},{6,5},{7,6},{0,7},{9,8},{10,9},{11,1... | collective-permute-start | bytes 27656 | tf_op jit(solution)/shard_map/ppermute | solution.py:25
  47.4 7.2 %collective-permute-start.6 = (f32[3,1,2,3,128]{4,3,2,1,0:T(4,128)S(1)}, f32[3,1,2,3,128]{4,3,2,1,0:T(4,128)S(1)}, u32[]{:S(2)}, u32[]{:S(2)}) collective-permute-start(f32[3,1,2,3,128]{4,3,2,1,0:T(4,128)S(1)} %pad_maximum_fusion.17), channel_id=1, source_target_pairs={{0,1},{1,2},{2,3},{3,4},{4,5},{5,6},{6,7},{7,0},{8,9},{9,10},{10,1... | collective-permute-start | bytes 27656 | tf_op jit(solution)/shard_map/ppermute | solution.py:24
  63.2 3.6 collective-permute-start.9
  65.2 4.5 collective-permute-start.8
  69.7 23.3 %collective-permute-start.11 = (f32[3,1,2,3,128]{4,3,2,1,0:T(4,128)S(1)}, f32[3,1,2,3,128]{4,3,2,1,0:T(4,128)S(1)}, u32[]{:S(2)}, u32[]{:S(2)}) collective-permute-start(f32[3,1,2,3,128]{4,3,2,1,0:T(4,128)S(1)} %pad_maximum_fusion.18), channel_id=1, source_target_pairs={{1,0},{2,1},{3,2},{4,3},{5,4},{6,5},{7,6},{0,7},{9,8},{10,9},{11,1... | collective-permute-start | bytes 27656 | tf_op jit(solution)/shard_map/ppermute | solution.py:25
  71.7 21.3 %collective-permute-start.10 = (f32[3,1,2,3,128]{4,3,2,1,0:T(4,128)S(1)}, f32[3,1,2,3,128]{4,3,2,1,0:T(4,128)S(1)}, u32[]{:S(2)}, u32[]{:S(2)}) collective-permute-start(f32[3,1,2,3,128]{4,3,2,1,0:T(4,128)S(1)} %pad_maximum_fusion.18), channel_id=1, source_target_pairs={{0,1},{1,2},{2,3},{3,4},{4,5},{5,6},{6,7},{7,0},{8,9},{9,10},{10,1... | collective-permute-start | bytes 27656 | tf_op jit(solution)/shard_map/ppermute | solution.py:24
  73.1 29.1 %copy-start.15 = (f32[256,512]{1,0:T(8,128)}, f32[256,512]{1,0:T(8,128)S(1)}, u32[]{:S(2)}) copy-start(f32[256,512]{1,0:T(8,128)S(1)} %get-tuple-element.153) | copy-start | bytes 1572868
  118.1 6.6 %collective-permute-start.16 = (f32[2,36,256]{2,1,0:T(8,128)S(1)}, f32[2,36,256]{2,1,0:T(8,128)S(1)}, u32[]{:S(2)}, u32[]{:S(2)}) collective-permute-start(f32[2,36,256]{2,1,0:T(8,128)S(1)} %slice.183), channel_id=1, source_target_pairs={{0,8},{8,16},{16,24},{24,0},{1,9},{9,17},{17,25},{25,1},{2,10},{10... | collective-permute-start | bytes 221192 | tf_op jit(solution)/shard_map/ppermute | solution.py:24
  121.7 5.0 collective-permute-start.17
  126.9 4.6 collective-permute-start.18
  126.9 4.6 collective-permute-start.19
  160.2 56.8 %all-to-all-start = ((f32[8,1,65536]{2,1,0:T(1,128)}), f32[8,1,65536]{2,1,0:T(1,128)}, u32[]{:S(2)}, u32[]{:S(2)}) async-start(f32[8,1,65536]{2,1,0:T(1,128)} %all_to_all.32), calls=%async_computation | async-start | bytes 4194304 | tf_op jit(solution)/shard_map/all_to_all | solution.py:328
  263.2 30.0 %all-to-all-start.1 = ((f32[4,1,131072]{2,1,0:T(1,128)}), f32[4,1,131072]{2,1,0:T(1,128)}, u32[]{:S(2)}, u32[]{:S(2)}) async-start(f32[4,1,131072]{2,1,0:T(1,128)} %all_to_all.33), calls=%async_computation.1 | async-start | bytes 4194304 | tf_op jit(solution)/shard_map/all_to_all | solution.py:338
  411.7 52.7 %all-to-all-start.3 = ((f32[8,1,65536]{2,1,0:T(1,128)}), f32[8,1,65536]{2,1,0:T(1,128)}, u32[]{:S(2)}, u32[]{:S(2)}) async-start(f32[8,1,65536]{2,1,0:T(1,128)} %all_to_all.35), calls=%async_computation.3 | async-start | bytes 4194304 | tf_op jit(solution)/shard_map/all_to_all | solution.py:362
  419.3 3.6 collective-permute-start.13
  420.8 4.5 collective-permute-start.12
  425.3 14.3 %collective-permute-start.15 = (f32[3,1,2,3,128]{4,3,2,1,0:T(4,128)S(1)}, f32[3,1,2,3,128]{4,3,2,1,0:T(4,128)S(1)}, u32[]{:S(2)}, u32[]{:S(2)}) collective-permute-start(f32[3,1,2,3,128]{4,3,2,1,0:T(4,128)S(1)} %pad_maximum_fusion.19), channel_id=1, source_target_pairs={{1,0},{2,1},{3,2},{4,3},{5,4},{6,5},{7,6},{0,7},{9,8},{10,9},{11,1... | collective-permute-start | bytes 27656 | tf_op jit(solution)/shard_map/ppermute | solution.py:25
  425.3 28.8 %collective-permute-start.14 = (f32[3,1,2,3,128]{4,3,2,1,0:T(4,128)S(1)}, f32[3,1,2,3,128]{4,3,2,1,0:T(4,128)S(1)}, u32[]{:S(2)}, u32[]{:S(2)}) collective-permute-start(f32[3,1,2,3,128]{4,3,2,1,0:T(4,128)S(1)} %pad_maximum_fusion.19), channel_id=1, source_target_pairs={{0,1},{1,2},{2,3},{3,4},{4,5},{5,6},{6,7},{7,0},{8,9},{9,10},{10,1... | collective-permute-start | bytes 27656 | tf_op jit(solution)/shard_map/ppermute | solution.py:24
  489.4 5.2 collective-permute-start.20
  490.0 5.0 collective-permute-start.21
  495.0 4.6 collective-permute-start.22
  497.2 2.9 collective-permute-start.23
  518.3 54.4 %copy-start.22 = (f32[3,512]{0,1:T(8,128)S(1)}, f32[3,512]{0,1:T(8,128)}, u32[]{:S(2)}) copy-start(f32[3,512]{0,1:T(8,128)} %copy.337) | copy-start | bytes 18436
  518.3 58.6 %copy-start.19 = (f32[3,4,128]{0,2,1:T(8,128)S(1)}, f32[3,4,128]{0,2,1:T(8,128)}, u32[]{:S(2)}) copy-start(f32[3,4,128]{0,2,1:T(8,128)} %copy-done.18) | copy-start | bytes 18436
  518.3 61.3 %copy-start.1 = (f32[512]{0:T(512)S(1)}, f32[512]{0:T(512)}, u32[]{:S(2)}) copy-start(f32[512]{0:T(512)} %param.18) | copy-start | bytes 6148
  (31 other events, 194.4 us)
where the time goes:
time: 590 us; the launch traced here: 580 us
  local copies, waits for them, and re-layouts  153 us (26%)
  waiting for transfers between devices  125 us (21%)
  other arithmetic  94.7 us (16%)
  matrix products  80.3 us (14%)
  blocking collectives  77.2 us (13%)
  starting transfers between devices  45.8 us (8%)
    psum x1, blocking collectives, local(): search_total = lax.psum(search_dot, ('slab', 'space'))  47.2 us
    all_to_all x1, waiting for transfers between devices, local(): lax.all_to_all(along_z.reshape(n_space, -1), 'space', split_axis=0, conca...  45.5 us
    all_to_all x1, blocking collectives, local(): lax.all_to_all(back_x.reshape(n_slab, -1), 'slab', split_axis=0, concat_a...  30 us
    ppermute x12, waiting for transfers between devices, with_halo(): before = lax.ppermute(last, axis, up)  28.9 us
    all_to_all x1, waiting for transfers between devices, local(): lax.all_to_all(along_y.reshape(n_slab, -1), 'slab', split_axis=0, concat_...  24.1 us
    ppermute x12, waiting for transfers between devices, with_halo(): after = lax.ppermute(initial, axis, down)  17.6 us
    reshape x2, local copies, waits for them, and re-layouts, local(): columns = columns.reshape(n_space, extent_x, extent_y, extent_k)  16.5 us
    dot_general x1, matrix products, local(): jnp.einsum('txkw,twsv->sxvk', returned, cas_table.reshape(n_slab, extent_...  16 us
  transfers between devices with their start and end apart: 27, of which 20 were waited for; matrix products, arithmetic and copies ran while one was open for 7% of the time, Pallas kernels for 0%

commit v1 on v0

--- a/solution.py
+++ b/solution.py
@@ -1,8 +1,11 @@
+import functools
 import math
 
 import jax
 import jax.numpy as jnp
 from jax import lax
+from jax.experimental import pallas as pl
+from jax.experimental.pallas import tpu as pltpu
 from jax.sharding import PartitionSpec as P
 
 G = 256
@@ -194,17 +197,6 @@
     return fields.reshape((count_tiles,) + fields.shape[2:])
 
 
-def fold_rims(padded, axis_id, length):
-    core = lax.slice_in_dim(padded, 4, length + 4, axis=axis_id)
-    lower_rim = lax.slice_in_dim(padded, 0, 2, axis=axis_id)
-    upper_rim = lax.slice_in_dim(padded, length + 6, length + 8, axis=axis_id)
-    lower_pad = [(0, 0)] * padded.ndim
-    lower_pad[axis_id] = (0, length - 2)
-    upper_pad = [(0, 0)] * padded.ndim
-    upper_pad[axis_id] = (length - 2, 0)
-    return core + jnp.pad(lower_rim, lower_pad) + jnp.pad(upper_rim, upper_pad)
-
-
 def to_tiles(values, count_tiles):
     return values.reshape(values.shape[0], count_tiles, -1).transpose(1, 0, 2)
 
@@ -215,10 +207,6 @@
 
 def tile_rims(payload):
     return with_halo(payload, (("slab", 0), ("space", 1)), 1)
-
-
-def grid_rims(values):
-    return with_halo(values, (("slab", 0), ("space", 1)), 2)
 
 
 def pool_from(received):
@@ -227,17 +215,155 @@
     return picked.reshape((-1,) + received.shape[3:])
 
 
-def point_tables(cell_row, frac_row, length, wrapped):
+NT = (((1,), (1,)), ((), ()))
+NN = (((1,), (0,)), ((), ()))
+
+
+def dot3(left, right, dims):
+    def halves(value):
+        high = value.astype(jnp.bfloat16)
+        return high, (value - high.astype(jnp.float32)).astype(jnp.bfloat16)
+
+    left_high, left_low = halves(left)
+    right_high, right_low = halves(right)
+    dot = functools.partial(
+        lax.dot_general, dimension_numbers=dims, preferred_element_type=jnp.float32
+    )
+    return dot(left_high, right_high) + (dot(left_high, right_low) + dot(left_low, right_high))
+
+
+def window_tables(cell_row, frac_row, length):
     weights, slopes = spline(frac_row)
-    step_ids = jnp.arange(5, dtype=jnp.int32)[:, None]
-    if wrapped:
-        targets = (cell_row[None] + step_ids - 2 + length) % length
-    else:
-        targets = cell_row[None] + step_ids
-    matches = (jnp.arange(length, dtype=jnp.int32)[:, None, None] == targets[None]).astype(
-        jnp.float32
-    )
-    return (jnp.sum(matches * weights[None], 1), jnp.sum(matches * slopes[None], 1))
+    offsets = lax.broadcasted_iota(jnp.int32, (length, cell_row.shape[1]), 0) - cell_row
+    weight_table = jnp.zeros(offsets.shape, jnp.float32)
+    slope_table = jnp.zeros(offsets.shape, jnp.float32)
+    for step in range(5):
+        matched = offsets == step
+        weight_table = jnp.where(matched, weights[step], weight_table)
+        slope_table = jnp.where(matched, slopes[step], slope_table)
+    return weight_table, slope_table
+
+
+def spread_kernel(cell_ref, frac_ref, search_ref, wave_ref, slope_wave_ref, cas_ref, out_ref):
+    width_u, width_v = out_ref.shape[2], cas_ref.shape[1]
+    freqs = wave_ref.shape[1]
+    weight_x, slope_x = window_tables(cell_ref[0, 0:1], frac_ref[0, 0:1], width_u)
+    weight_y, slope_y = window_tables(cell_ref[0, 1:2], frac_ref[0, 1:2], width_v)
+    along_x = jnp.concatenate([slope_x, weight_x], 1)
+    moved_x = search_ref[0, 0:1]
+    moved_y = search_ref[0, 1:2]
+    moved_z = search_ref[0, 2:3]
+    rows = []
+    for k in range(freqs):
+        wave = wave_ref[0, k : k + 1]
+        slope_wave = slope_wave_ref[0, k : k + 1]
+        rows.append(
+            jnp.concatenate(
+                [
+                    weight_y * (moved_x * wave),
+                    slope_y * (moved_y * wave) + weight_y * (moved_z * slope_wave),
+                ],
+                1,
+            )
+        )
+    spread = dot3(jnp.concatenate(rows, 0), along_x, NT)
+    turned = jnp.concatenate(
+        [spread[k * width_v : (k + 1) * width_v].T for k in range(freqs)], 0
+    )
+    along_y = dot3(turned, cas_ref[0], NN).reshape(freqs, width_u, -1)
+
+    @pl.when(pl.program_id(1) == 0)
+    def _():
+        out_ref[:, 0] = along_y
+
+    @pl.when(pl.program_id(1) > 0)
+    def _():
+        out_ref[:, 0] += along_y
+
+
+def scale_kernel(planes_ref, cas_ref, turned_ref, factor_ref, out_ref, energy_ref):
+    spectrum = dot3(turned_ref[...], planes_ref[0], NN)
+    scaled = spectrum * factor_ref[0]
+    energy = jnp.sum(scaled * spectrum, 0, keepdims=True)
+    energy_ref[0] = jnp.broadcast_to(energy, energy_ref.shape[1:])
+    out_ref[0] = dot3(cas_ref[...], scaled, NN)
+
+
+def probe_kernel(cell_ref, frac_ref, planes_ref, wave_ref, slope_wave_ref, cas_ref, out_ref):
+    width_u, width_v = planes_ref.shape[2], cas_ref.shape[1]
+    freqs = wave_ref.shape[1]
+    atoms = cell_ref.shape[2]
+    weight_x, slope_x = window_tables(cell_ref[0, 0:1], frac_ref[0, 0:1], width_u)
+    weight_y, slope_y = window_tables(cell_ref[0, 1:2], frac_ref[0, 1:2], width_v)
+    along_x = jnp.concatenate([slope_x, weight_x], 1)
+    planes = jnp.concatenate([dot3(cas_ref[0], planes_ref[k, 0], NT) for k in range(freqs)], 0)
+    probed = dot3(planes, along_x, NN)
+    field_x = jnp.zeros((1, atoms), jnp.float32)
+    field_y = field_x
+    field_z = field_x
+    for k in range(freqs):
+        wave = wave_ref[0, k : k + 1]
+        slope_wave = slope_wave_ref[0, k : k + 1]
+        block = probed[k * width_v : (k + 1) * width_v]
+        with_slope = block[:, :atoms]
+        with_weight = block[:, atoms:]
+        field_x += wave * jnp.sum(with_slope * weight_y, 0, keepdims=True)
+        field_y += wave * jnp.sum(with_weight * slope_y, 0, keepdims=True)
+        field_z += slope_wave * jnp.sum(with_weight * weight_y, 0, keepdims=True)
+    out_ref[0, 0:1] = field_x
+    out_ref[0, 1:2] = field_y
+    out_ref[0, 2:3] = field_z
+
+
+def z_waves(cell_z, frac_z, freq_z):
+    weights, slopes = spline(frac_z)
+    turns = 2.0 * math.pi / G
+    angle = turns * (cell_z[:, None] * freq_z[None, :, None] % G).astype(jnp.float32)
+    cosine, sine = jnp.cos(angle), jnp.sin(angle)
+    first = turns * freq_z.astype(jnp.float32)[None, :, None]
+
+    def combined(values):
+        values = values[:, :, None]
+        even = (
+            values[2]
+            + (values[1] + values[3]) * jnp.cos(first)
+            + (values[0] + values[4]) * jnp.cos(2.0 * first)
+        )
+        odd = (values[3] - values[1]) * jnp.sin(first) + (values[4] - values[0]) * jnp.sin(
+            2.0 * first
+        )
+        return (cosine + sine) * even + (cosine - sine) * odd
+
+    return combined(weights), combined(slopes)
+
+
+def padded_length(length):
+    return -(-length // 8) * 8
+
+
+def window_rows(blocks, length):
+    width = length + 4
+    starts = length * jnp.arange(blocks, dtype=jnp.int32)[:, None]
+    spots = jnp.arange(padded_length(width), dtype=jnp.int32)[None]
+    points = (starts + spots - 2 + G) % G
+    angles = (
+        2.0
+        * math.pi
+        / G
+        * (points[:, :, None] * jnp.arange(G, dtype=jnp.int32) % G).astype(jnp.float32)
+    )
+    return jnp.where((spots < width)[:, :, None], jnp.cos(angles) + jnp.sin(angles), 0.0)
+
+
+def spread_to_all(values):
+    devices = lax.axis_size("slab") * lax.axis_size("space")
+    copies = jnp.broadcast_to(values[None], (devices,) + values.shape)
+    return lax.all_to_all(copies, ("slab", "space"), split_axis=0, concat_axis=0, tiled=True)
+
+
+def exchange_sum(fields):
+    moved = lax.all_to_all(fields, ("slab", "space"), split_axis=0, concat_axis=0, tiled=True)
+    return jnp.sum(moved, 0)
 
 
 def local(
@@ -262,15 +388,18 @@
     n_space = lax.axis_size("space")
     extent_x = G // n_slab
     extent_y = G // n_space
-    extent_k = G // n_space
-    extent_w = G // n_slab
-    slab_index = lax.axis_index("slab")
-    space_index = lax.axis_index("space")
+    freqs = G // (n_slab * n_space)
+    first_freq = (lax.axis_index("slab") * n_space + lax.axis_index("space")) * freqs
+    freq_z = first_freq + jnp.arange(freqs, dtype=jnp.int32)
     cell_rows = cells[:, atom_order]
     frac_rows = fraction[:, atom_order]
     alphas = polarizability[atom_order][None]
     target = residual[:, atom_order]
     moments = dipoles[:, atom_order]
+    places_all = spread_to_all(jnp.concatenate([cell_rows.astype(jnp.float32), frac_rows], 0))
+    cells_all = places_all[:, :3].astype(jnp.int32)
+    frac_all = places_all[:, 3:]
+    wave_z, slope_wave_z = z_waves(cells_all[:, 2], frac_all[:, 2], freq_z)
     positions = cell_rows.astype(jnp.float32) + frac_rows
     geometry = to_tiles(jnp.concatenate([positions, alphas], 0), count_tiles)
     shift_rows = []
@@ -302,87 +431,77 @@
     search = alphas * (target + short_from(search_tiles, first_pool[:, 4:]))
     for sweep_id in range(2):
         search = alphas * (target + short_apply(search))
-    search_dot = jnp.sum(target * search)
-    search_total = lax.psum(search_dot, ("slab", "space"))
-    weight_x, slope_x = point_tables(cell_rows[0], frac_rows[0], extent_x + 4, False)
-    weight_y, slope_y = point_tables(cell_rows[1], frac_rows[1], extent_y + 4, False)
-    weight_z, slope_z = point_tables(cell_rows[2], frac_rows[2], G, True)
-    plane_xs = (slope_x[:, None] * weight_y[None]).reshape(-1, atom_count)
-    plane_ys = (weight_x[:, None] * slope_y[None]).reshape(-1, atom_count)
-    plane_ww = (weight_x[:, None] * weight_y[None]).reshape(-1, atom_count)
-    left_side = jnp.concatenate(
-        [search[0][None] * plane_xs + search[1][None] * plane_ys, plane_ww], 1
-    )
-    right_side = jnp.concatenate([weight_z.T, (search[2][None] * slope_z).T], 0)
-    spread = jnp.dot(left_side, right_side, precision=HIGHEST).reshape(
-        extent_x + 4, extent_y + 4, G
-    )
-    planes = fold_rims(fold_rims(grid_rims(spread), 0, extent_x), 1, extent_y)
+    search_all = spread_to_all(search)
+    window_x = window_rows(n_slab, extent_x).reshape(-1, G)
+    window_y = window_rows(n_space, extent_y)
+    width_u = padded_length(extent_x + 4)
+    width_v = padded_length(extent_y + 4)
     grid_ids = jnp.arange(G, dtype=jnp.int32)
-    angles = 2.0 * math.pi / G * (grid_ids[:, None] * grid_ids[None, :] % G).astype(jnp.float32)
-    cas_table = jnp.cos(angles) + jnp.sin(angles)
-    freq_z = space_index * extent_k + jnp.arange(extent_k, dtype=jnp.int32)
-    along_z = jnp.einsum(
-        "xvz,zsk->sxvk", planes, cas_table.reshape(G, n_space, extent_k), precision=HIGHEST
-    )
-    columns = lax.all_to_all(
-        along_z.reshape(n_space, -1), "space", split_axis=0, concat_axis=0, tiled=True
-    )
-    columns = columns.reshape(n_space, extent_x, extent_y, extent_k)
-    along_y = jnp.einsum(
-        "sxvk,svtw->txkw",
-        columns,
-        cas_table.reshape(n_space, extent_y, n_slab, extent_w),
-        precision=HIGHEST,
-    )
-    gathered_x = lax.all_to_all(
-        along_y.reshape(n_slab, -1), "slab", split_axis=0, concat_axis=0, tiled=True
-    )
-    gathered_x = gathered_x.reshape(n_slab, extent_x, extent_k, extent_w)
-    spectrum = jnp.einsum(
-        "txkw,txm->kwm", gathered_x, cas_table.reshape(n_slab, extent_x, G), precision=HIGHEST
-    )
-    freq_y = slab_index * extent_w + jnp.arange(extent_w, dtype=jnp.int32)
-    scaled = spectrum * multiplier(
-        grid_ids[None, None, :], freq_y[None, :, None], freq_z[:, None, None]
-    )
-    back_x = jnp.einsum(
-        "kwm,txm->txkw", scaled, cas_table.reshape(n_slab, extent_x, G), precision=HIGHEST
-    )
-    returned = lax.all_to_all(
-        back_x.reshape(n_slab, -1), "slab", split_axis=0, concat_axis=0, tiled=True
-    )
-    returned = returned.reshape(n_slab, extent_x, extent_k, extent_w)
-    planes_send = jnp.einsum(
-        "txkw,twsv->sxvk",
-        returned,
-        cas_table.reshape(n_slab, extent_w, n_space, extent_y),
-        precision=HIGHEST,
-    )
-    planes_back = lax.all_to_all(
-        planes_send.reshape(n_space, -1), "space", split_axis=0, concat_axis=0, tiled=True
-    )
-    planes_back = planes_back.reshape(n_space, extent_x, extent_y, extent_k)
-    potential = jnp.einsum(
-        "sxvk,skz->xvz", planes_back, cas_table.reshape(n_space, extent_k, G), precision=HIGHEST
-    )
-    beside_all = grid_rims(potential)
-    probed = jnp.dot(
-        beside_all.reshape(-1, G), jnp.concatenate([weight_z, slope_z], 1), precision=HIGHEST
-    )
-    probed_w = probed[:, :atom_count]
-    probed_s = probed[:, atom_count:]
-    recip_field = -jnp.stack(
-        [
-            jnp.sum(plane_xs * probed_w, 0),
-            jnp.sum(plane_ys * probed_w, 0),
-            jnp.sum(plane_ww * probed_s, 0),
-        ]
-    )
-    applied = search / alphas - short_apply(search) - SELF_FIELD * search - recip_field
-    curve_local = jnp.sum(search * applied)
-    curve_total = lax.psum(curve_local, ("slab", "space"))
-    step_size = search_total / curve_total
+    factor = multiplier(
+        grid_ids[None, :, None], grid_ids[None, None, :], freq_z[:, None, None]
+    )
+
+    def per_block(rows):
+        return pl.BlockSpec((1, rows, atom_count), lambda s, q: (s * n_space + q, 0, 0))
+
+    planes_spec = pl.BlockSpec((freqs, 1, width_u, G), lambda s, q: (0, s, 0, 0))
+    cas_spec = pl.BlockSpec((1, width_v, G), lambda s, q: (q, 0, 0))
+    along_y = pl.pallas_call(
+        spread_kernel,
+        grid=(n_slab, n_space),
+        in_specs=[
+            per_block(3),
+            per_block(3),
+            per_block(3),
+            per_block(freqs),
+            per_block(freqs),
+            cas_spec,
+        ],
+        out_specs=planes_spec,
+        out_shape=jax.ShapeDtypeStruct((freqs, n_slab, width_u, G), jnp.float32),
+        name="spread",
+    )(cells_all, frac_all, search_all, wave_z, slope_wave_z, window_y)
+    whole = pl.BlockSpec((1, G, G), lambda k: (k, 0, 0))
+    planes = pl.BlockSpec((1, n_slab * width_u, G), lambda k: (k, 0, 0))
+    back_x, energy = pl.pallas_call(
+        scale_kernel,
+        grid=(freqs,),
+        in_specs=[
+            planes,
+            pl.BlockSpec(window_x.shape, lambda k: (0, 0)),
+            pl.BlockSpec(window_x.shape[::-1], lambda k: (0, 0)),
+            whole,
+        ],
+        out_specs=[planes, pl.BlockSpec((1, 8, G), lambda k: (k, 0, 0))],
+        out_shape=[
+            jax.ShapeDtypeStruct((freqs, n_slab * width_u, G), jnp.float32),
+            jax.ShapeDtypeStruct((freqs, 8, G), jnp.float32),
+        ],
+        name="scale",
+    )(along_y.reshape(freqs, -1, G), window_x, window_x.T, factor)
+    direct = search / alphas - short_apply(search) - SELF_FIELD * search
+    partial_sums = jnp.stack(
+        [jnp.sum(target * search), jnp.sum(search * direct) + jnp.sum(energy[:, 0])]
+    )
+    totals = jnp.sum(spread_to_all(jnp.broadcast_to(partial_sums[:, None], (2, 128)))[:, :, 0], 0)
+    step_size = totals[0] / totals[1]
+    fields = pl.pallas_call(
+        probe_kernel,
+        grid=(n_slab, n_space),
+        in_specs=[
+            per_block(3),
+            per_block(3),
+            planes_spec,
+            per_block(freqs),
+            per_block(freqs),
+            cas_spec,
+        ],
+        out_specs=per_block(3),
+        out_shape=jax.ShapeDtypeStruct(cells_all.shape, jnp.float32),
+        name="probe",
+    )(cells_all, frac_all, back_x.reshape(along_y.shape), wave_z, slope_wave_z, window_y)
+    mine = exchange_sum(fields)
+    applied = direct + mine
 
     def restore(values):
         return jnp.zeros_like(values).at[:, atom_order].set(values)

time: 590 us -> 264 us (0.45)
  local copies, waits for them, and re-layouts: 153 us -> 37 us
  waiting for transfers between devices: 125 us -> 14.3 us
  Pallas kernels: 0 us -> 103 us
  matrix products: 80.3 us -> 0 us
  blocking collectives: 77.2 us -> 0 us
  other arithmetic: 94.7 us -> 52.1 us
    pallas_call x0 -> x3, Pallas kernels: none -> 103 us  [the longest x1 54.7 us: local(): pl.pallas_call(spread_kernel, grid=(n_slab, n_space), in_specs=[per_block...]
    dot_general x8 -> x0, matrix products: 80.3 us -> none  [the longest x1 16 us: local(): jnp.einsum('txkw,twsv->sxvk', returned, cas_table.reshape(n_slab, extent_...]
    all_to_all x3 -> x4, waiting for transfers between devices: 78.7 us -> 4.18 us  [the longest x3 2.19 us: spread_to_all(): lax.all_to_all(copies, ('slab', 'space'), split_axis=0, concat_axis=0, ti...]
    psum x1 -> x0, blocking collectives: 47.2 us -> none  [local(): search_total = lax.psum(search_dot, ('slab', 'space'))]
    reshape x7 -> x0, local copies, waits for them, and re-layouts: 42.3 us -> none  [the longest x2 16.5 us: local(): columns = columns.reshape(n_space, extent_x, extent_y, extent_k)]
    all_to_all x4 -> x0, other arithmetic: 32.5 us -> none  [the longest x1 8.39 us: local(): lax.all_to_all(back_x.reshape(n_slab, -1), 'slab', split_axis=0, concat_a...]
    all_to_all x1 -> x0, blocking collectives: 30 us -> none  [local(): lax.all_to_all(back_x.reshape(n_slab, -1), 'slab', split_axis=0, concat_a...]
    all_to_all x4 -> x0, local copies, waits for them, and re-layouts: 28.1 us -> none  [the longest x1 8.58 us: local(): lax.all_to_all(planes_send.reshape(n_space, -1), 'space', split_axis=0, c...]
  transfers between devices with their start and end apart: 27 -> 20, of which waited for: 20 -> 10; matrix products, arithmetic and copies ran while one was open for 7% -> 25% of each run, Pallas kernels for 0% -> 15%
where the time goes in v1:
time: 264 us; the launch traced here: 259 us
  Pallas kernels  103 us (39%)
  other arithmetic  52.1 us (20%)
  starting transfers between devices  49.1 us (19%)
  local copies, waits for them, and re-layouts  37 us (14%)
  waiting for transfers between devices  14.3 us (5%)
  between operations  4.25 us (2%)
    pallas_call x1, Pallas kernels, local(): pl.pallas_call(spread_kernel, grid=(n_slab, n_space), in_specs=[per_block...  54.7 us
    pallas_call x1, Pallas kernels, local(): pl.pallas_call(probe_kernel, grid=(n_slab, n_space), in_specs=[per_block(...  38.3 us
    all_to_all x3, starting transfers between devices, spread_to_all(): lax.all_to_all(copies, ('slab', 'space'), split_axis=0, concat_axis=0, ti...  22.5 us
    reduce_sum x4, other arithmetic, short_per_tile(): projection = jnp.sum(displacement * dipole[:, :, None, :], 1)  14.4 us
    ppermute x8, starting transfers between devices, with_halo(): before = lax.ppermute(last, axis, up)  11.9 us
    pallas_call x1, Pallas kernels, local(): pl.pallas_call(scale_kernel, grid=(freqs,), in_specs=[planes, pl.BlockSpe...  9.67 us
    unnamed x57, local copies, waits for them, and re-layouts  9.6 us
    mul x2, other arithmetic, pair_per_tile(): return (weight_pair * rank_five, weight_pair * rank_three)  9.06 us
  transfers between devices with their start and end apart: 20, of which 10 were waited for; matrix products, arithmetic and copies ran while one was open for 25% of the time, Pallas kernels for 15%

profile of v1, /device:TPU:12, one launch (start us, length us, event | category | flops | bytes accessed | tf_op | source)
XLA Modules:
  0.0 259.3 jit_solution(17602669473338173963)
XLA Ops:
  5.3 3.5 %gather_fusion.2 = f32[512]{0:T(512)S(1)} fusion(f32[512]{0:T(512)S(1)} %copy-done, s32[1024]{0:T(1024)S(1)} %pad_clamp_fusion.3), kind=kCustom, calls=%fused_computation.2 | custom fusion | bytes 6144 | tf_op jit(solution)/shard_map/gather | solution.py:396
  14.9 5.1 %all-to-all-start = ((f32[32,6,512]{2,1,0:T(8,128)}), f32[32,6,512]{2,1,0:T(8,128)S(1)}, u32[]{:S(2)}, u32[]{:S(2)}) async-start(f32[32,6,512]{2,1,0:T(8,128)} %broadcast_in_dim.215), calls=%async_computation | async-start | bytes 1048576 | tf_op jit(solution)/shard_map/all_to_all | solution.py:361
  21.0 2.4 add_select_fusion.4.turned_ref
  23.5 2.3 fusion.3.factor_ref
  27.6 2.4 collective-permute-done.2
  32.5 2.2 slice.181
  35.8 3.3 %multiply_reduce_fusion.3 = (f32[4,8,128,128]{3,2,1,0:T(8,128)S(1)}, f32[4,8,128,128]{3,2,1,0:T(8,128)S(1)}) fusion(f32[4,8,3,128]{3,2,1,0:T(4,128)S(1)} %bitcast.163, f32[4,8,1,128,128]{4,3,2,1,0:T(8,128)S(1)} %fusion.13, f32[4,8,2,128,128]{4,3,2,1,0:T(8,128)} %slice.181), kind=kLoop, calls=%fused_computation.29 | loop fusion | flops 6815744 | bytes 10534912 | tf_op jit(solution)/shard_map/while/body/eval_jaxpr/vmap()/reduce_sum | solution.py:178
  39.1 7.3 %fusion.7 = (f32[4,8,128,128]{3,2,1,0:T(8,128)S(1)}, f32[4,8,128,128]{3,2,1,0:T(8,128)S(1)}) fusion(f32[4,8,128,128]{3,2,1,0:T(8,128)S(1)} %get-tuple-element.142, f32[4,8,128]{2,1,0:T(8,128)S(1)} %bitcast.184, f32[4,128]{1,0:T(4,128)S(1)} %bitcast.210, f32[128,128]{1,0:T(8,128)S(1)} %fusion.58, f32[4,8]{1,0:T(4,128)S(1)} %get-tuple-element.188, ...), kind=kLoop, calls=%fused_computation.46 | loop fusion | flops 46661632 | bytes 6375680 | tf_op jit(solution)/shard_map/while/body/eval_jaxpr/vmap()/mul | solution.py:149
  46.4 1.8 fusion.6
  49.9 2.0 subtract_reduce_fusion.3
  55.5 2.1 add_select_fusion.5.cas_ref
  57.6 3.6 %collective-permute-start.6 = (f32[3,1,2,3,128]{4,3,2,1,0:T(4,128)S(1)}, f32[3,1,2,3,128]{4,3,2,1,0:T(4,128)S(1)}, u32[]{:S(2)}, u32[]{:S(2)}) collective-permute-start(f32[3,1,2,3,128]{4,3,2,1,0:T(4,128)S(1)} %pad_maximum_fusion.13), channel_id=1, source_target_pairs={{0,1},{1,2},{2,3},{3,4},{4,5},{5,6},{6,7},{7,0},{8,9},{9,10},{10,1... | collective-permute-start | bytes 27656 | tf_op jit(solution)/shard_map/ppermute | solution.py:27
  61.3 2.0 add_select_fusion.6.cas_ref
  64.6 3.7 %multiply_reduce_fusion.2 = f32[4,8,128,128]{3,2,1,0:T(8,128)S(1)} fusion(f32[4,8,3,128]{3,2,1,0:T(4,128)S(1)} %bitcast.167, f32[4,8,1,128,128]{4,3,2,1,0:T(8,128)S(1)} %fusion.13, f32[4,8,2,128,128]{4,3,2,1,0:T(8,128)} %slice.181), kind=kLoop, calls=%fused_computation.27 | loop fusion | flops 4194304 | bytes 8437760 | tf_op jit(solution)/shard_map/while/body/eval_jaxpr/vmap()/reduce_sum | solution.py:178
  69.3 2.0 subtract_reduce_fusion.2
  81.9 3.7 %multiply_reduce_fusion.1 = f32[4,8,128,128]{3,2,1,0:T(8,128)S(1)} fusion(f32[4,8,3,128]{3,2,1,0:T(4,128)S(1)} %bitcast.169, f32[4,8,1,128,128]{4,3,2,1,0:T(8,128)S(1)} %fusion.13, f32[4,8,2,128,128]{4,3,2,1,0:T(8,128)} %slice.181), kind=kLoop, calls=%fused_computation.25 | loop fusion | flops 4194304 | bytes 8437760 | tf_op jit(solution)/shard_map/while/body/eval_jaxpr/vmap()/reduce_sum | solution.py:178
  86.6 2.0 subtract_reduce_fusion.1
  89.2 1.7 collective-permute-start.12
  99.0 3.7 %multiply_reduce_fusion = f32[4,8,128,128]{3,2,1,0:T(8,128)S(1)} fusion(f32[4,8,3,128]{3,2,1,0:T(4,128)S(1)} %bitcast.165, f32[4,8,1,128,128]{4,3,2,1,0:T(8,128)S(1)} %fusion.13, f32[4,8,2,128,128]{4,3,2,1,0:T(8,128)} %slice.181), kind=kLoop, calls=%fused_computation.23 | loop fusion | flops 4194304 | bytes 8437760 | tf_op jit(solution)/shard_map/while/body/eval_jaxpr/vmap()/reduce_sum | solution.py:178
  103.7 2.0 subtract_reduce_fusion
  107.0 12.6 %all-to-all-start.1 = ((f32[32,3,512]{2,1,0:T(4,128)}), f32[32,3,512]{2,1,0:T(4,128)S(1)}, u32[]{:S(2)}, u32[]{:S(2)}) async-start(f32[32,3,512]{2,1,0:T(4,128)} %broadcast_in_dim.216), calls=%async_computation.1 | async-start | bytes 524288 | tf_op jit(solution)/shard_map/all_to_all | solution.py:361
  122.0 3.5 %multiply_add_fusion.1 = (f32[32,8,512]{2,1,0:T(8,128)}, f32[32,8,512]{2,1,0:T(8,128)}) fusion(f32[32,512]{1,0:T(8,128)S(1)} %get-tuple-element.189, f32[32,512]{1,0:T(8,128)S(1)} %get-tuple-element.201, f32[32,512]{1,0:T(8,128)S(1)} %get-tuple-element.190, f32[32,512]{1,0:T(8,128)S(1)} %get-tuple-element.191, f32[32,512]{1,0:T(8,128)S(1)} %get-tuple-element.181, ...), kind=kLoop, calls=%fused_computation.81 | loop fusion | flops 4718592 | bytes 1769632 | tf_op jit(solution)/shard_map/add | solution.py:335
  125.5 2.2 all-to-all-done.1.search_ref
  128.4 54.7 %spread.1 = f32[8,4,72,256]{3,2,1,0:T(8,128)} custom-call(s32[32,3,512]{2,1,0:T(4,128)} %copy-done.13, f32[32,3,512]{2,1,0:T(4,128)} %get-tuple-element.177.frac_ref, f32[32,3,512]{2,1,0:T(4,128)} %copy-done.14, f32[32,8,512]{2,1,0:T(8,128)} %get-tuple-element.180.wave_ref, f32[32,8,512]{2,1,0:T(8,128)} %get-tuple-element.179.slope_wave_ref, ...), custom_call_target="tpu_custom_call" | custom-call | tf_op jit(solution)/shard_map/spread/pallas_call | solution.py:449
  183.1 9.7 %scale.1 = (f32[8,288,256]{2,1,0:T(8,128)}, f32[8,8,256]{2,1,0:T(8,128)}) custom-call(f32[8,288,256]{2,1,0:T(8,128)} %bitcast.159, f32[288,256]{1,0:T(8,128)} %add_select_fusion.6.cas_ref, f32[256,288]{1,0:T(8,128)} %add_select_fusion.4.turned_ref, f32[8,256,256]{2,1,0:T(8,128)} %fusion.3.factor_ref), custom_call_target="tpu_custom_call" | custom-call | tf_op jit(solution)/shard_map/scale/pallas_call | solution.py:466
  196.9 4.8 %all-to-all-start.2 = ((f32[32,2,128]{2,1,0:T(2,128)}), f32[32,2,128]{2,1,0:T(2,128)S(1)}, u32[]{:S(2)}, u32[]{:S(2)}) async-start(f32[32,2,128]{2,1,0:T(2,128)} %broadcast_in_dim_broadcast_in_dim_broadcast_in_dim.2), calls=%async_computation.2 | async-start | bytes 65536 | tf_op jit(solution)/shard_map/all_to_all | solution.py:361
  201.8 38.3 %probe.1 = f32[32,3,512]{2,1,0:T(4,128)} custom-call(s32[32,3,512]{2,1,0:T(4,128)} %copy-done.13, f32[32,3,512]{2,1,0:T(4,128)} %get-tuple-element.177.frac_ref, f32[8,4,72,256]{3,2,1,0:T(8,128)} %bitcast.160, f32[32,8,512]{2,1,0:T(8,128)} %get-tuple-element.180.wave_ref, f32[32,8,512]{2,1,0:T(8,128)} %get-tuple-element.179.slope_wave_ref, ...), custom_call_target="tpu_custom_call" | custom-call | tf_op jit(solution)/shard_map/probe/pallas_call | solution.py:488
  240.0 5.8 %all-to-all-start.3 = ((f32[32,3,512]{2,1,0:T(4,128)}), f32[32,3,512]{2,1,0:T(4,128)S(1)}, u32[]{:S(2)}, u32[]{:S(2)}) async-start(f32[32,3,512]{2,1,0:T(4,128)} %probe.1), calls=%async_computation.3 | async-start | bytes 524288 | tf_op jit(solution)/shard_map/all_to_all | solution.py:365
  247.4 1.8 scatter_custom_fusion.2
  251.9 2.0 all-to-all-done.3
  254.2 1.8 scatter_custom_fusion.1
  256.8 1.8 scatter_custom_fusion
  (201 shorter events, 57.3 us)
Async XLA Ops:
  0.6 4.7 %copy-start = (f32[512]{0:T(512)S(1)}, f32[512]{0:T(512)}, u32[]{:S(2)}) copy-start(f32[512]{0:T(512)} %param.18) | copy-start | bytes 6148
  0.6 8.2 %copy-start.15 = (f32[3,512]{1,0:T(4,128)S(1)}, f32[3,512]{1,0:T(4,128)}, u32[]{:S(2)}) copy-start(f32[3,512]{1,0:T(4,128)} %param.15) | copy-start | bytes 18436
  2.2 8.0 %copy-start.21 = (s32[1,2]{1,0:T(1,128)S(1)}, s32[1,2]{1,0:T(1,128)}, u32[]{:S(2)}) copy-start(s32[1,2]{1,0:T(1,128)} %param.20) | copy-start | bytes 28
  8.8 11.4 %copy-start.19 = (s32[8]{0:T(128)S(1)}, s32[8]{0:T(128)}, u32[]{:S(2)}) copy-start(s32[8]{0:T(128)} %constant.424) | copy-start | bytes 100
  8.9 11.4 %copy-start.17 = (s32[1,4,8]{2,1,0:T(4,128)S(1)}, s32[1,4,8]{2,1,0:T(4,128)}, u32[]{:S(2)}) copy-start(s32[1,4,8]{2,1,0:T(4,128)} %param.21) | copy-start | bytes 388
  8.9 11.5 %copy-start.20 = (s32[1,4]{1,0:T(1,128)S(1)}, s32[1,4]{1,0:T(1,128)}, u32[]{:S(2)}) copy-start(s32[1,4]{1,0:T(1,128)} %param.22) | copy-start | bytes 52
  10.8 14.9 %collective-permute-start = (f32[1,1,2,7,128]{4,3,2,1,0:T(8,128)S(1)}, f32[1,1,2,7,128]{4,3,2,1,0:T(8,128)S(1)}, u32[]{:S(2)}, u32[]{:S(2)}) collective-permute-start(f32[1,1,2,7,128]{4,3,2,1,0:T(8,128)S(1)} %bitcast.193), channel_id=1, source_target_pairs={{0,8},{8,16},{16,24},{24,0},{1,9},{9,17},{17,25},{25,1},{2,10},{10... | collective-permute-start | bytes 21512 | tf_op jit(solution)/shard_map/ppermute | solution.py:27
  12.4 13.4 %collective-permute-start.1 = (f32[1,1,2,7,128]{4,3,2,1,0:T(8,128)S(1)}, f32[1,1,2,7,128]{4,3,2,1,0:T(8,128)S(1)}, u32[]{:S(2)}, u32[]{:S(2)}) collective-permute-start(f32[1,1,2,7,128]{4,3,2,1,0:T(8,128)S(1)} %bitcast.194), channel_id=1, source_target_pairs={{8,0},{16,8},{24,16},{0,24},{9,1},{17,9},{25,17},{1,25},{10,2},{18... | collective-permute-start | bytes 21512 | tf_op jit(solution)/shard_map/ppermute | solution.py:28
  14.9 91.4 %all-to-all-start = ((f32[32,6,512]{2,1,0:T(8,128)}), f32[32,6,512]{2,1,0:T(8,128)S(1)}, u32[]{:S(2)}, u32[]{:S(2)}) async-start(f32[32,6,512]{2,1,0:T(8,128)} %broadcast_in_dim.215), calls=%async_computation | async-start | bytes 1048576 | tf_op jit(solution)/shard_map/all_to_all | solution.py:361
  20.0 10.7 %copy-start.18 = (f32[8,4]{1,0:T(8,128)S(1)}, f32[8,4]{1,0:T(8,128)}, u32[]{:S(2)}) copy-start(f32[8,4]{1,0:T(8,128)} %constant.414.clone) | copy-start | bytes 388
  25.8 4.3 %collective-permute-start.2 = (f32[3,1,2,7,128]{4,3,2,1,0:T(8,128)S(1)}, f32[3,1,2,7,128]{4,3,2,1,0:T(8,128)S(1)}, u32[]{:S(2)}, u32[]{:S(2)}) collective-permute-start(f32[3,1,2,7,128]{4,3,2,1,0:T(8,128)S(1)} %pad_maximum_fusion.10), channel_id=1, source_target_pairs={{0,1},{1,2},{2,3},{3,4},{4,5},{5,6},{6,7},{7,0},{8,9},{9,10},{10,1... | collective-permute-start | bytes 64520 | tf_op jit(solution)/shard_map/ppermute | solution.py:27
  25.9 4.1 %collective-permute-start.3 = (f32[3,1,2,7,128]{4,3,2,1,0:T(8,128)S(1)}, f32[3,1,2,7,128]{4,3,2,1,0:T(8,128)S(1)}, u32[]{:S(2)}, u32[]{:S(2)}) collective-permute-start(f32[3,1,2,7,128]{4,3,2,1,0:T(8,128)S(1)} %pad_maximum_fusion.10), channel_id=1, source_target_pairs={{1,0},{2,1},{3,2},{4,3},{5,4},{6,5},{7,6},{0,7},{9,8},{10,9},{11,1... | collective-permute-start | bytes 64520 | tf_op jit(solution)/shard_map/ppermute | solution.py:28
  52.5 5.1 %collective-permute-start.4 = (f32[1,1,2,3,128]{4,3,2,1,0:T(4,128)S(1)}, f32[1,1,2,3,128]{4,3,2,1,0:T(4,128)S(1)}, u32[]{:S(2)}, u32[]{:S(2)}) collective-permute-start(f32[1,1,2,3,128]{4,3,2,1,0:T(4,128)S(1)} %bitcast.197), channel_id=1, source_target_pairs={{0,8},{8,16},{16,24},{24,0},{1,9},{9,17},{17,25},{25,1},{2,10},{10... | collective-permute-start | bytes 9224 | tf_op jit(solution)/shard_map/ppermute | solution.py:27
  54.0 3.6 %collective-permute-start.5 = (f32[1,1,2,3,128]{4,3,2,1,0:T(4,128)S(1)}, f32[1,1,2,3,128]{4,3,2,1,0:T(4,128)S(1)}, u32[]{:S(2)}, u32[]{:S(2)}) collective-permute-start(f32[1,1,2,3,128]{4,3,2,1,0:T(4,128)S(1)} %bitcast.198), channel_id=1, source_target_pairs={{8,0},{16,8},{24,16},{0,24},{9,1},{17,9},{25,17},{1,25},{10,2},{18... | collective-permute-start | bytes 9224 | tf_op jit(solution)/shard_map/ppermute | solution.py:28
  57.6 5.7 %collective-permute-start.6 = (f32[3,1,2,3,128]{4,3,2,1,0:T(4,128)S(1)}, f32[3,1,2,3,128]{4,3,2,1,0:T(4,128)S(1)}, u32[]{:S(2)}, u32[]{:S(2)}) collective-permute-start(f32[3,1,2,3,128]{4,3,2,1,0:T(4,128)S(1)} %pad_maximum_fusion.13), channel_id=1, source_target_pairs={{0,1},{1,2},{2,3},{3,4},{4,5},{5,6},{6,7},{7,0},{8,9},{9,10},{10,1... | collective-permute-start | bytes 27656 | tf_op jit(solution)/shard_map/ppermute | solution.py:27
  61.3 2.0 collective-permute-start.7
  64.6 4.7 %copy-start.10 = (f32[4,8,128,128]{3,2,1,0:T(8,128)S(1)}, f32[4,8,128,128]{3,2,1,0:T(8,128)}, u32[]{:S(2)}) copy-start(f32[4,8,128,128]{3,2,1,0:T(8,128)} %copy-done.9) | copy-start | bytes 6291460
  71.9 4.5 %collective-permute-start.8 = (f32[1,1,2,3,128]{4,3,2,1,0:T(4,128)S(1)}, f32[1,1,2,3,128]{4,3,2,1,0:T(4,128)S(1)}, u32[]{:S(2)}, u32[]{:S(2)}) collective-permute-start(f32[1,1,2,3,128]{4,3,2,1,0:T(4,128)S(1)} %bitcast.201), channel_id=1, source_target_pairs={{0,8},{8,16},{16,24},{24,0},{1,9},{9,17},{17,25},{25,1},{2,10},{10... | collective-permute-start | bytes 9224 | tf_op jit(solution)/shard_map/ppermute | solution.py:27
  73.2 3.6 %collective-permute-start.9 = (f32[1,1,2,3,128]{4,3,2,1,0:T(4,128)S(1)}, f32[1,1,2,3,128]{4,3,2,1,0:T(4,128)S(1)}, u32[]{:S(2)}, u32[]{:S(2)}) collective-permute-start(f32[1,1,2,3,128]{4,3,2,1,0:T(4,128)S(1)} %bitcast.202), channel_id=1, source_target_pairs={{8,0},{16,8},{24,16},{0,24},{9,1},{17,9},{25,17},{1,25},{10,2},{18... | collective-permute-start | bytes 9224 | tf_op jit(solution)/shard_map/ppermute | solution.py:28
  76.8 3.1 %collective-permute-start.10 = (f32[3,1,2,3,128]{4,3,2,1,0:T(4,128)S(1)}, f32[3,1,2,3,128]{4,3,2,1,0:T(4,128)S(1)}, u32[]{:S(2)}, u32[]{:S(2)}) collective-permute-start(f32[3,1,2,3,128]{4,3,2,1,0:T(4,128)S(1)} %pad_maximum_fusion.14), channel_id=1, source_target_pairs={{0,1},{1,2},{2,3},{3,4},{4,5},{5,6},{6,7},{7,0},{8,9},{9,10},{10,1... | collective-permute-start | bytes 27656 | tf_op jit(solution)/shard_map/ppermute | solution.py:27
  77.8 2.8 %collective-permute-start.11 = (f32[3,1,2,3,128]{4,3,2,1,0:T(4,128)S(1)}, f32[3,1,2,3,128]{4,3,2,1,0:T(4,128)S(1)}, u32[]{:S(2)}, u32[]{:S(2)}) collective-permute-start(f32[3,1,2,3,128]{4,3,2,1,0:T(4,128)S(1)} %pad_maximum_fusion.14), channel_id=1, source_target_pairs={{1,0},{2,1},{3,2},{4,3},{5,4},{6,5},{7,6},{0,7},{9,8},{10,9},{11,1... | collective-permute-start | bytes 27656 | tf_op jit(solution)/shard_map/ppermute | solution.py:28
  81.9 4.7 %copy-start.11 = (f32[4,8,128,128]{3,2,1,0:T(8,128)S(1)}, f32[4,8,128,128]{3,2,1,0:T(8,128)}, u32[]{:S(2)}) copy-start(f32[4,8,128,128]{3,2,1,0:T(8,128)} %copy-done.9) | copy-start | bytes 6291460
  89.2 4.5 %collective-permute-start.12 = (f32[1,1,2,3,128]{4,3,2,1,0:T(4,128)S(1)}, f32[1,1,2,3,128]{4,3,2,1,0:T(4,128)S(1)}, u32[]{:S(2)}, u32[]{:S(2)}) collective-permute-start(f32[1,1,2,3,128]{4,3,2,1,0:T(4,128)S(1)} %bitcast.205), channel_id=1, source_target_pairs={{0,8},{8,16},{16,24},{24,0},{1,9},{9,17},{17,25},{25,1},{2,10},{10... | collective-permute-start | bytes 9224 | tf_op jit(solution)/shard_map/ppermute | solution.py:27
  90.9 3.6 %collective-permute-start.13 = (f32[1,1,2,3,128]{4,3,2,1,0:T(4,128)S(1)}, f32[1,1,2,3,128]{4,3,2,1,0:T(4,128)S(1)}, u32[]{:S(2)}, u32[]{:S(2)}) collective-permute-start(f32[1,1,2,3,128]{4,3,2,1,0:T(4,128)S(1)} %bitcast.206), channel_id=1, source_target_pairs={{8,0},{16,8},{24,16},{0,24},{9,1},{17,9},{25,17},{1,25},{10,2},{18... | collective-permute-start | bytes 9224 | tf_op jit(solution)/shard_map/ppermute | solution.py:28
  94.5 3.1 %collective-permute-start.14 = (f32[3,1,2,3,128]{4,3,2,1,0:T(4,128)S(1)}, f32[3,1,2,3,128]{4,3,2,1,0:T(4,128)S(1)}, u32[]{:S(2)}, u32[]{:S(2)}) collective-permute-start(f32[3,1,2,3,128]{4,3,2,1,0:T(4,128)S(1)} %pad_maximum_fusion.15), channel_id=1, source_target_pairs={{0,1},{1,2},{2,3},{3,4},{4,5},{5,6},{6,7},{7,0},{8,9},{9,10},{10,1... | collective-permute-start | bytes 27656 | tf_op jit(solution)/shard_map/ppermute | solution.py:27
  95.5 2.1 collective-permute-start.15
  99.0 4.7 %copy-start.12 = (f32[4,8,128,128]{3,2,1,0:T(8,128)S(1)}, f32[4,8,128,128]{3,2,1,0:T(8,128)}, u32[]{:S(2)}) copy-start(f32[4,8,128,128]{3,2,1,0:T(8,128)} %copy-done.9) | copy-start | bytes 6291460
  107.0 20.6 %all-to-all-start.1 = ((f32[32,3,512]{2,1,0:T(4,128)}), f32[32,3,512]{2,1,0:T(4,128)S(1)}, u32[]{:S(2)}, u32[]{:S(2)}) async-start(f32[32,3,512]{2,1,0:T(4,128)} %broadcast_in_dim.216), calls=%async_computation.1 | async-start | bytes 524288 | tf_op jit(solution)/shard_map/all_to_all | solution.py:361
  121.9 5.8 %copy-start.13 = (s32[32,3,512]{2,1,0:T(4,128)}, s32[32,3,512]{2,1,0:T(4,128)S(1)}, u32[]{:S(2)}) copy-start(s32[32,3,512]{2,1,0:T(4,128)S(1)} %get-tuple-element.178.cell_ref) | copy-start | bytes 589828
  196.9 43.1 %all-to-all-start.2 = ((f32[32,2,128]{2,1,0:T(2,128)}), f32[32,2,128]{2,1,0:T(2,128)S(1)}, u32[]{:S(2)}, u32[]{:S(2)}) async-start(f32[32,2,128]{2,1,0:T(2,128)} %broadcast_in_dim_broadcast_in_dim_broadcast_in_dim.2), calls=%async_computation.2 | async-start | bytes 65536 | tf_op jit(solution)/shard_map/all_to_all | solution.py:361
  201.7 44.1 %copy-start.16 = (f32[3,512]{1,0:T(4,128)S(1)}, f32[3,512]{1,0:T(4,128)}, u32[]{:S(2)}) copy-start(f32[3,512]{1,0:T(4,128)} %param.14) | copy-start | bytes 18436
  240.0 13.9 %all-to-all-start.3 = ((f32[32,3,512]{2,1,0:T(4,128)}), f32[32,3,512]{2,1,0:T(4,128)S(1)}, u32[]{:S(2)}, u32[]{:S(2)}) async-start(f32[32,3,512]{2,1,0:T(4,128)} %probe.1), calls=%async_computation.3 | async-start | bytes 524288 | tf_op jit(solution)/shard_map/all_to_all | solution.py:365
  (10 other events, 33.2 us)
